TPU v7x, 32 devices: a whole 2x2x4 slice. The times are simulated.
32 devices in a mesh: head: 4 (over z), batch: 8 (over y, x, core).
Axes of the slice: x: 2, y: 2, z: 4, core: 2. Of those that a mesh axis runs over, the one named last changes fastest.
Arguments:
- window_ids: int32 [32, 22], replicated, may hold values from 0 to 64127
- pool_ids: int32 [32, 64, 3], replicated, may hold values from 0 to 64127
- guess_index: int32 [32, 7], replicated, may hold values from 0 to 63
- lengths: int32 [32], P('batch'), may hold values from 16 to 2048, as said below
- embed_table: bfloat16 [64128, 8192], P('batch', 'head'), may hold values from -6 to 6
- w_query: bfloat16 [8192, 8192], P('batch', 'head'), may hold values from -0.0625 to 0.0625
- w_key: bfloat16 [8192, 1024], P('batch', 'head'), may hold values from -0.0625 to 0.0625
- w_value: bfloat16 [8192, 1024], P('batch', 'head'), may hold values from -0.0625 to 0.0625
- k_cache: bfloat16 [8, 32, 2048, 128], P(None, None, ('head', 'batch')), may hold values from -300 to 300
- v_cache: bfloat16 [8, 32, 2048, 128], P(None, None, ('head', 'batch')), may hold values from -12 to 12
Outputs:
- attended: bfloat16 [1376, 8192], P('batch', 'head')
- k_decode: bfloat16 [8, 32, 2048, 128], P('head', 'batch')
- v_decode: bfloat16 [8, 32, 2048, 128], P('head', 'batch')
Inputs may be any that keep to these rules, and one draw needn't show every extreme that they name: `lengths`: in every draw one sequence has exactly 2048 cached tokens.
All inputs are finite; a program needn't handle non-finite values.
Results may differ from a plain program's by a relative error of at most 0.0055.
The roundings to bfloat16 on the way count: a program that leaves them out, or rounds other values in their place, can miss the bound.
Values may be sent and summed in bfloat16 or wider, within the bound.
No kernel may reach another device: no remote copies, remote signals or barrier semaphores. Data moves between devices by JAX's collectives and lax.ppermute only.
A program may use at most 192 MiB of HBM per device.

v0:
```python
import jax
import jax.numpy as jnp
import numpy as np
from jax import lax
from jax.sharding import PartitionSpec as P

W = 7
NG = 4
G = 7
ROPE_BASE = 500000.0
NORM_EPS = 1e-05


def layout_tables():
    levels = NG - 1
    level_of = np.repeat(np.arange(levels), W)
    column_of = np.tile(np.arange(W), levels)
    window_mask = (level_of[None, :] == 0) & (column_of[None, :] <= column_of[:, None]) | (
        column_of[None, :] == column_of[:, None]
    ) & (level_of[None, :] <= level_of[:, None])
    guess_of = np.repeat(np.arange(G), levels)
    slot_of = np.tile(np.arange(levels), G)
    guess_mask = (guess_of[None, :] == guess_of[:, None]) & (slot_of[None, :] <= slot_of[:, None])
    window_rows = levels * W
    total_rows = 1 + window_rows + G * levels
    allowed = np.zeros((total_rows, total_rows), np.bool_)
    allowed[:, 0] = True
    allowed[1 : 1 + window_rows, 1 : 1 + window_rows] = window_mask
    allowed[1 + window_rows :, 1 + window_rows :] = guess_mask
    offsets = np.concatenate(
        [
            np.zeros(1, np.int32),
            (1 + level_of + column_of).astype(np.int32),
            (1 + slot_of).astype(np.int32),
        ]
    )
    return (offsets, allowed)


def gather_ids(window_ids, pool_ids, guess_index):
    wanted = jnp.broadcast_to(
        guess_index[:, :, None], (guess_index.shape[0], guess_index.shape[1], pool_ids.shape[2])
    )
    picked = jnp.take_along_axis(pool_ids, wanted, axis=1)
    return jnp.concatenate([window_ids, picked.reshape(picked.shape[0], -1)], axis=1)


def rotate(vectors, positions):
    head_dim = vectors.shape[-1]
    half_dim = head_dim // 2
    ladder = jnp.arange(half_dim).astype(jnp.float32)
    frequencies = jnp.power(ROPE_BASE, ladder * (-2.0 / head_dim))
    angles = positions.astype(jnp.float32)[..., None] * frequencies
    cosine = jnp.cos(angles)[..., None, :]
    sines = jnp.sin(angles)[..., None, :]
    front_half = vectors[..., :half_dim]
    second = vectors[..., half_dim:]
    return jnp.concatenate(
        [front_half * cosine - second * sines, second * cosine + front_half * sines], axis=-1
    )


def per_device(
    window_ids,
    pool_ids,
    guess_index,
    lengths,
    embed_table,
    w_query,
    w_key,
    w_value,
    k_cache,
    v_cache,
):
    offsets, allowed = layout_tables()
    total_rows = offsets.shape[0]
    n_head = lax.axis_size("head")
    n_batch = lax.axis_size("batch")
    kv_total, seq_total, slab, head_dim = k_cache.shape
    kv_dev = kv_total // n_head
    seq_dev = seq_total // n_batch
    token_ids = gather_ids(window_ids, pool_ids, guess_index).reshape(-1)
    vocab_rows = embed_table.shape[0]
    local_ids = token_ids - lax.axis_index("batch") * vocab_rows
    inside = (local_ids >= 0) & (local_ids < vocab_rows)
    found_rows = jnp.take(embed_table, jnp.clip(local_ids, 0, vocab_rows - 1), axis=0)
    partial_rows = jnp.where(inside[:, None], found_rows.astype(jnp.float32), 0.0)
    embedded = lax.psum_scatter(
        partial_rows.astype(jnp.bfloat16), "batch", scatter_dimension=0, tiled=True
    )
    embedded = lax.all_gather(embedded, "head", axis=1, tiled=True)
    widened = embedded.astype(jnp.float32)
    normed = (
        widened * lax.rsqrt(jnp.mean(widened * widened, axis=-1, keepdims=True) + NORM_EPS)
    ).astype(jnp.bfloat16)
    pieces = (
        lax.all_gather(w_query, "batch", axis=0, tiled=True),
        lax.all_gather(w_key, "batch", axis=0, tiled=True),
        lax.all_gather(w_value, "batch", axis=0, tiled=True),
    )
    query_raw, key_raw, value_raw = tuple(
        (jnp.dot(normed, piece_part, preferred_element_type=jnp.float32) for piece_part in pieces)
    )
    q_heads = w_query.shape[1] // head_dim
    per_group = q_heads // kv_dev
    positions = lengths[:, None] + jnp.asarray(offsets).astype(jnp.int32)[None, :]
    queries = rotate(query_raw.reshape(seq_dev, total_rows, q_heads, head_dim), positions).astype(
        jnp.bfloat16
    )
    keys_new = rotate(key_raw.reshape(seq_dev, total_rows, kv_dev, head_dim), positions).astype(
        jnp.bfloat16
    )
    values_new = value_raw.astype(jnp.bfloat16).reshape(seq_dev, total_rows, kv_dev, head_dim)

    def arrange(kv_block):
        shaped = kv_block.reshape(n_head, kv_dev, n_batch, seq_dev, slab, head_dim)
        return jnp.swapaxes(shaped, 1, 2)

    context = slab * n_head * n_batch
    flat_k = arrange(k_cache).reshape(n_head * n_batch, kv_dev, seq_dev, slab, head_dim)
    flat_v = arrange(v_cache).reshape(n_head * n_batch, kv_dev, seq_dev, slab, head_dim)
    k_here, v_here = (
        lax.all_to_all(flat_k, ("head", "batch"), split_axis=0, concat_axis=3, tiled=True),
        lax.all_to_all(flat_v, ("head", "batch"), split_axis=0, concat_axis=3, tiled=True),
    )
    k_here = k_here.reshape(kv_dev, seq_dev, context, head_dim)
    v_here = v_here.reshape(kv_dev, seq_dev, context, head_dim)
    q_five = queries.reshape(seq_dev, total_rows, kv_dev, per_group, head_dim)
    score_scale = head_dim ** (-0.5)
    old_scores = (
        jnp.einsum("stkgd,kscd->skgtc", q_five, k_here, preferred_element_type=jnp.float32)
        * score_scale
    )
    new_scores = (
        jnp.einsum("stkgd,sukd->skgtu", q_five, keys_new, preferred_element_type=jnp.float32)
        * score_scale
    )
    visible = jnp.arange(context)[None, :] < lengths[:, None]
    old_scores = jnp.where(visible[:, None, None, None, :], old_scores, -1e30)
    new_scores = jnp.where(jnp.asarray(allowed), new_scores, -1e30)
    row_peak = jnp.maximum(
        jnp.max(old_scores, axis=-1, keepdims=True), jnp.max(new_scores, axis=-1, keepdims=True)
    )
    old_powers = jnp.exp(old_scores - row_peak)
    new_powers = jnp.exp(new_scores - row_peak)
    denominator = jnp.sum(old_powers, axis=-1, keepdims=True) + jnp.sum(
        new_powers, axis=-1, keepdims=True
    )
    old_weights = (old_powers / denominator).astype(jnp.bfloat16)
    new_weights = (new_powers / denominator).astype(jnp.bfloat16)
    blended = jnp.einsum(
        "skgtc,kscd->stkgd", old_weights, v_here, preferred_element_type=jnp.float32
    )
    blended = blended + jnp.einsum(
        "skgtu,sukd->stkgd", new_weights, values_new, preferred_element_type=jnp.float32
    )
    attended = blended.astype(jnp.bfloat16).reshape(seq_dev * total_rows, q_heads * head_dim)
    return (attended, k_here, v_here)


def solution(mesh):
    placed = (
        P(),
        P(),
        P(),
        P("batch"),
        P("batch", "head"),
        P("batch", "head"),
        P("batch", "head"),
        P("batch", "head"),
        P(None, None, ("head", "batch"), None),
        P(None, None, ("head", "batch"), None),
    )
    return jax.shard_map(
        per_device,
        mesh=mesh,
        in_specs=placed,
        out_specs=(
            P("batch", "head"),
            P("head", "batch", None, None),
            P("head", "batch", None, None),
        ),
        check_vma=False,
    )
```

profile of v0, /device:TPU:0, one launch (start us, length us, event | category | flops | bytes accessed | tf_op | source)
XLA Modules:
  0.0 621.6 jit_solution(6536742778525920510)
XLA Ops:
  7.2 0.7 broadcast_add_fusion
  7.9 0.8 copy.112
  8.7 0.7 broadcast_compare_fusion
  9.4 0.1 copy.111
  9.5 0.1 copy.110
  9.6 0.2 shift-left_or_fusion
  9.7 0.2 reshape.206
  10.0 9.1 %gather_fusion.1 = s32[672]{0:T(1024)S(1)} fusion(s32[32,64,3]{1,0,2:T(8,128)S(1)} %copy-done, s32[672]{0:T(1024)S(1)} %reshape.206), kind=kCustom, calls=%fused_computation.1 | custom fusion | bytes 13440 | tf_op jit(solution)/shard_map/jit(take_along_axis)/gather | solution.py:44
  19.0 0.2 reshape.209
  19.2 0.2 fusion.16
  19.4 0.1 reshape.216
  19.7 0.1 min.18
  19.8 0.1 min.16
  20.0 0.1 and.29
  20.2 56.0 %gather_fusion = bf16[1376,2048]{1,0:T(8,128)(2,1)} fusion(bf16[8016,2048]{1,0:T(8,128)(2,1)} %param.16, s32[2048]{0:T(1024)S(1)} %pad_clamp_fusion), kind=kCustom, calls=%fused_computation | custom fusion | bytes 11277696 | tf_op jit(solution)/shard_map/jit(_take)/gather | solution.py:86
  76.2 7.0 %select_convert_fusion = bf16[1376,2048]{1,0:T(8,128)(2,1)} fusion(bf16[1376,2048]{1,0:T(8,128)(2,1)} %gather_fusion, pred[1376]{0:T(1024)(128)(4,1)S(1)} %compare_and_fusion.1, pred[1376]{0:T(1024)(128)(4,1)S(1)} %and.29), kind=kLoop, calls=%fused_computation.8 | loop fusion | flops 11272192 | bytes 11274944 | tf_op jit(solution)/shard_map/convert_element_type | solution.py:89
  83.2 60.9 %fusion = bf16[176,2048]{1,0:T(8,128)(2,1)S(1)} fusion(bf16[1376,2048]{1,0:T(8,128)(2,1)} %select_convert_fusion), kind=kCustom, calls=%all-reduce-scatter | all-reduce-scatter fusion | flops 2883585 | bytes 6357504
  144.1 1.3 collective-permute-start
  145.5 0.6 dynamic-slice.4
  146.7 1.5 concatenate.25
  148.2 1.0 constant_dynamic-slice_fusion
  149.3 0.7 all-gather.9.cloned.1.call-update
  150.0 0.7 all-gather.11.cloned.1.call-update
  150.8 0.5 all-gather.7.cloned.1.call-update
  151.3 5.6 copy.121
  156.9 10.1 %all-to-all-start = ((bf16[32,2,4,64,128]{4,3,1,2,0:T(8,128)(2,1)}), bf16[32,2,4,64,128]{4,3,1,2,0:T(8,128)(2,1)}, u32[]{:S(2)}, u32[]{:S(2)}) async-start(bf16[32,2,4,64,128]{4,3,1,2,0:T(8,128)(2,1)} %bitcast.80), calls=%async_computation | async-start | bytes 8388608 | tf_op jit(solution)/shard_map/all_to_all | solution.py:123
  167.0 5.6 copy.130
  172.6 130.5 %all-to-all-done = bf16[32,2,4,64,128]{4,3,1,2,0:T(8,128)(2,1)} async-done(((bf16[32,2,4,64,128]{4,3,1,2,0:T(8,128)(2,1)}), bf16[32,2,4,64,128]{4,3,1,2,0:T(8,128)(2,1)}, u32[]{:S(2)}, u32[]{:S(2)}) %all-to-all-start) | async-done | bytes 4194336 | tf_op jit(solution)/shard_map/all_to_all | solution.py:123
  303.1 3.9 all-to-all-start.1
  307.1 0.4 multiply_cosine_fusion
  307.6 2.6 fusion.4
  310.2 28.7 %all-gather.9.cloned.1.call-done = bf16[8192,256]{1,0:T(8,128)(2,1)} async-done(((bf16[1024,256]{1,0:T(8,128)(2,1)}), bf16[8192,256]{1,0:T(8,128)(2,1)}) %all-gather.9.cloned.1.call-update) | async-done | bytes 4194320 | tf_op jit(solution)/shard_map/all_gather | solution.py:98
  338.9 4.0 fusion.25
  343.0 0.1 reshape.192
  343.1 57.4 %all-gather.11.cloned.1.call-done = bf16[8192,256]{1,0:T(8,128)(2,1)} async-done(((bf16[1024,256]{1,0:T(8,128)(2,1)}), bf16[8192,256]{1,0:T(8,128)(2,1)}) %all-gather.11.cloned.1.call-update) | async-done | bytes 4194320 | tf_op jit(solution)/shard_map/all_gather | solution.py:99
  400.5 3.1 convolution_convert_fusion
  403.7 0.3 fusion.29
  404.0 6.0 copy.122
  410.0 4.2 copy.131
  414.2 0.8 copy-done.2
  415.0 2.7 copy.135
  417.7 0.5 copy-done.4
  418.2 2.3 copy.136
  420.5 141.8 %all-gather.7.cloned.1.call-done = bf16[8192,2048]{1,0:T(8,128)(2,1)} async-done(((bf16[1024,2048]{1,0:T(8,128)(2,1)}), bf16[8192,2048]{1,0:T(8,128)(2,1)}) %all-gather.7.cloned.1.call-update) | async-done | bytes 33554448 | tf_op jit(solution)/shard_map/all_gather | solution.py:97
  562.3 13.7 %fusion.27 = f32[172,2048]{1,0:T(8,128)S(1)} fusion(bf16[8192,2048]{1,0:T(8,128)(2,1)} %all-gather.7.cloned.1.call-done, bf16[172,8192]{1,0:T(8,128)(2,1)S(1)} %copy-done.5, f32[172]{0:T(256)S(1)} %add_rsqrt_fusion), kind=kOutput, calls=%fused_computation.63 | convolution fusion | flops 5775589376 | bytes 37782192 | tf_op jit(solution)/shard_map/dot_general | solution.py:102
  576.1 0.3 copy.148
  576.3 0.1 slice.26
  576.4 0.7 fusion.11
  577.1 0.4 pad_maximum_fusion
  577.5 1.0 copy-done.3
  578.5 9.3 %bitcast_reduce_fusion = (f32[4,2,8,43]{2,3,1,0:T(8,128)S(1)}, f32[4,2,43,8,2048]{4,3,2,1,0:T(8,128)}) fusion(pred[4,2048]{1,0:T(4,128)(4,1)S(1)} %iota_compare_fusion, bf16[2,4,2048,128,1]{3,2,4,0,1:T(8,128)(2,1)S(1)} %bitcast.76, bf16[4,43,2,8,128]{4,3,2,1,0:T(8,128)(2,1)S(1)} %pad_maximum_fusion), kind=kOutput, calls=%fused_computation.3 | convolution fusion | flops 1459746048 | bytes 27462400 | tf_op jit(solution)/shard_map/stkgd,kscd->skgtc/dot_general | solution.py:131
  587.8 0.1 copy.126
  588.0 1.0 fusion.30
  589.0 0.1 copy.127
  589.2 0.4 fusion.8
  589.6 10.9 %fusion.2 = f32[4,2,8,43]{2,3,1,0:T(8,128)S(1)} fusion(f32[4,2,43,8,2048]{4,3,2,1,0:T(8,128)} %get-tuple-element.27, f32[4,2,8,43]{2,3,1,0:T(8,128)S(1)} %copy.127, pred[4,2048]{1,0:T(4,128)(4,1)S(1)} %iota_compare_fusion), kind=kLoop, calls=%fused_computation.7 | loop fusion | flops 22541632 | bytes 22574592 | tf_op jit(solution)/shard_map/reduce_sum | solution.py:146
  600.4 0.1 copy.128
  600.6 0.4 divide_convert_fusion.2
  600.9 0.1 copy.129
  601.1 0.6 copy.133
  601.7 11.5 %fusion.7 = f32[4,43,2,8,128]{4,3,1,2,0:T(8,128)S(1)} fusion(bf16[2,4,2048,128,1]{3,2,4,0,1:T(8,128)(2,1)} %bitcast.78, f32[4,2,43,8,2048]{4,3,2,1,0:T(8,128)} %get-tuple-element.27, f32[4,2,8,43]{2,3,1,0:T(8,128)S(1)} %copy.129, f32[4,2,8,43]{2,3,1,0:T(8,128)S(1)} %copy.127, pred[4,2048]{1,0:T(4,128)(4,1)S(1)} %iota_compare_fusion), kind=kOutput, calls=%fused_computation.19 | convolution fusion | flops 1471021056 | bytes 28177920 | tf_op jit(solution)/shard_map/skgtc,kscd->stkgd/dot_general | solution.py:151
  613.2 0.5 fusion.9
  613.7 0.1 copy.134
  613.9 1.2 reshape.197
  (42 shorter events, 0.8 us)
Async XLA Ops:
  7.2 2.8 copy-start
  7.2 300.4 %all-gather.5.cloned.1.call-start = ((), (), s32[]{:S(2)}) async-start(), calls=%async_computation.2 | async-start | bytes 3604480 | tf_op jit(solution)/shard_map/all_gather | solution.py:91
  10.0 9.6 %copy-start.6 = (s32[32,22]{0,1:T(8,128)S(1)}, s32[32,22]{0,1:T(8,128)}, u32[]{:S(2)}) copy-start(s32[32,22]{0,1:T(8,128)} %param.12) | copy-start | bytes 8452
  83.2 62.3 %copy-start.9 = (u32[32]{0:T(128)S(1)}, u32[32]{0:T(128)}, u32[]{:S(2)}) copy-start(u32[32]{0:T(128)} %constant.86) | copy-start | bytes 388
  144.1 2.6 collective-permute-start
  149.2 189.7 %all-gather.9.cloned.1.call-start = ((), (), s32[]{:S(2)}) async-start(), calls=%async_computation.4 | async-start | bytes 4718592 | tf_op jit(solution)/shard_map/all_gather | solution.py:98
  150.0 250.5 %all-gather.11.cloned.1.call-start = ((), (), s32[]{:S(2)}) async-start(), calls=%async_computation.5 | async-start | bytes 4718592 | tf_op jit(solution)/shard_map/all_gather | solution.py:99
  150.7 411.6 %all-gather.7.cloned.1.call-start = ((), (), s32[]{:S(2)}) async-start(), calls=%async_computation.3 | async-start | bytes 37748736 | tf_op jit(solution)/shard_map/all_gather | solution.py:97
  156.9 146.2 %all-to-all-start = ((bf16[32,2,4,64,128]{4,3,1,2,0:T(8,128)(2,1)}), bf16[32,2,4,64,128]{4,3,1,2,0:T(8,128)(2,1)}, u32[]{:S(2)}, u32[]{:S(2)}) async-start(bf16[32,2,4,64,128]{4,3,1,2,0:T(8,128)(2,1)} %bitcast.80), calls=%async_computation | async-start | bytes 8388608 | tf_op jit(solution)/shard_map/all_to_all | solution.py:123
  303.1 3.9 copy-start.8
  303.1 3.9 copy-start.10
  303.1 106.9 %all-to-all-start.1 = ((bf16[32,2,4,64,128]{4,3,1,2,0:T(8,128)(2,1)}), bf16[32,2,4,64,128]{4,3,1,2,0:T(8,128)(2,1)}, u32[]{:S(2)}, u32[]{:S(2)}) async-start(bf16[32,2,4,64,128]{4,3,1,2,0:T(8,128)(2,1)} %bitcast.79), calls=%async_computation.1 | async-start | bytes 8388608 | tf_op jit(solution)/shard_map/all_to_all | solution.py:124
  310.2 90.3 %copy-start.5 = (bf16[172,8192]{1,0:T(8,128)(2,1)S(1)}, bf16[172,8192]{1,0:T(8,128)(2,1)}, u32[]{:S(2)}) copy-start(bf16[172,8192]{1,0:T(8,128)(2,1)} %all-gather.5.cloned.1.call-done) | copy-start | bytes 8454148
  410.0 5.0 copy-start.2
  414.2 4.0 copy-start.4
  576.3 2.2 copy-start.3
  578.5 9.4 %copy-start.7 = (pred[43,43]{0,1:T(8,128)(4,1)S(1)}, pred[43,43]{0,1:T(8,128)(4,1)}, u32[]{:S(2)}) copy-start(pred[43,43]{0,1:T(8,128)(4,1)} %constant.63.clone) | copy-start | bytes 5551
  601.7 13.4 %copy-start.1 = (s32[32,64,3]{1,0,2:T(8,128)S(1)}, s32[32,64,3]{1,0,2:T(8,128)}, u32[]{:S(2)}) copy-start(s32[32,64,3]{1,0,2:T(8,128)} %param.13) | copy-start | bytes 73732
Sparse Core Ops, SparseCore 0:
  149.4 121.8 all-gather.4
  273.2 65.6 all-gather.8
  340.8 59.6 all-gather.10
  402.2 160.0 all-gather.6
where the time goes:
time: 623 us; the launch traced here: 622 us
  waiting for transfers between devices  360 us (58%)
  local copies, waits for them, and re-layouts  102 us (16%)
  blocking collectives  60.9 us (10%)
  matrix products  43.3 us (7%)
  other arithmetic  24.8 us (4%)
  starting transfers between devices  15.4 us (2%)
  between operations  14.8 us (2%)
    all_gather x1, waiting for transfers between devices, per_device(): lax.all_gather(w_query, 'batch', axis=0, tiled=True)  142 us
    all_to_all x1, waiting for transfers between devices, per_device(): lax.all_to_all(flat_k, ('head', 'batch'), split_axis=0, concat_axis=3, ti...  130 us
    unnamed x1, blocking collectives  60.9 us
    all_gather x1, waiting for transfers between devices, per_device(): lax.all_gather(w_value, 'batch', axis=0, tiled=True)  57.4 us
    gather x1, local copies, waits for them, and re-layouts, per_device(): jnp.take(embed_table, jnp.clip(local_ids, 0, vocab_rows - 1), axis=0)  56 us
    all_gather x1, waiting for transfers between devices, per_device(): lax.all_gather(w_key, 'batch', axis=0, tiled=True)  28.7 us
    dot_general x3, matrix products, per_device(): jnp.dot(normed, piece_part, preferred_element_type=jnp.float32)  20.9 us
  transfers between devices with their start and end apart: 7, of which 4 were waited for; matrix products, arithmetic and copies ran while one was open for 6% of the time, Pallas kernels for 0%

commit v1 on v0

--- a/solution.py
+++ b/solution.py
@@ -120,7 +120,15 @@
     flat_k = arrange(k_cache).reshape(n_head * n_batch, kv_dev, seq_dev, slab, head_dim)
     flat_v = arrange(v_cache).reshape(n_head * n_batch, kv_dev, seq_dev, slab, head_dim)
     k_here, v_here = (
-        lax.all_to_all(flat_k, ("head", "batch"), split_axis=0, concat_axis=3, tiled=True),
+        jnp.concatenate(
+            lax.all_to_all(
+                jnp.stack(jnp.split(flat_k, lax.axis_size(("head", "batch")), axis=0)),
+                ("head", "batch"),
+                0,
+                0,
+            ),
+            axis=3,
+        ),
         lax.all_to_all(flat_v, ("head", "batch"), split_axis=0, concat_axis=3, tiled=True),
     )
     k_here = k_here.reshape(kv_dev, seq_dev, context, head_dim)

time: 623 us -> 602 us (0.966)
  waiting for transfers between devices: 360 us -> 325 us
  local copies, waits for them, and re-layouts: 102 us -> 118 us
    all_gather x1, waiting for transfers between devices: 28.7 us -> 0.02 us  [per_device(): lax.all_gather(w_key, 'batch', axis=0, tiled=True)]
    all_to_all x1, waiting for transfers between devices: 0.01 us -> 20.3 us  [per_device(): lax.all_to_all(flat_v, ('head', 'batch'), split_axis=0, concat_axis=3, ti...]
    unnamed x32 -> x65, local copies, waits for them, and re-layouts: 11.6 us -> 31.6 us
    all_to_all x1, waiting for transfers between devices: 130 us -> 112 us  [per_device(): lax.all_to_all(jnp.stack(jnp.split(flat_k, lax.axis_size(('head', 'batch'...]
    all_gather x1, waiting for transfers between devices: 142 us -> 132 us  [per_device(): lax.all_gather(w_query, 'batch', axis=0, tiled=True)]
  transfers between devices with their start and end apart: 7 -> 7, of which waited for: 4 -> 4; matrix products, arithmetic and copies ran while one was open for 6% -> 9% of each run, Pallas kernels for 0% -> 0%
where the time goes in v1:
time: 602 us; the launch traced here: 601 us
  waiting for transfers between devices  325 us (54%)
  local copies, waits for them, and re-layouts  118 us (20%)
  blocking collectives  60.9 us (10%)
  matrix products  44.4 us (7%)
  other arithmetic  22.8 us (4%)
  starting transfers between devices  15.4 us (3%)
  between operations  14.8 us (2%)
    all_gather x1, waiting for transfers between devices, per_device(): lax.all_gather(w_query, 'batch', axis=0, tiled=True)  132 us
    all_to_all x1, waiting for transfers between devices, per_device(): lax.all_to_all(jnp.stack(jnp.split(flat_k, lax.axis_size(('head', 'batch'...  112 us
    unnamed x1, blocking collectives  60.9 us
    all_gather x1, waiting for transfers between devices, per_device(): lax.all_gather(w_value, 'batch', axis=0, tiled=True)  58 us
    gather x1, local copies, waits for them, and re-layouts, per_device(): jnp.take(embed_table, jnp.clip(local_ids, 0, vocab_rows - 1), axis=0)  56 us
    unnamed x65, local copies, waits for them, and re-layouts  31.6 us
    dot_general x3, matrix products, per_device(): jnp.dot(normed, piece_part, preferred_element_type=jnp.float32)  21.2 us
    all_to_all x1, waiting for transfers between devices, per_device(): lax.all_to_all(flat_v, ('head', 'batch'), split_axis=0, concat_axis=3, ti...  20.3 us
  transfers between devices with their start and end apart: 7, of which 4 were waited for; matrix products, arithmetic and copies ran while one was open for 9% of the time, Pallas kernels for 0%

profile of v1, /device:TPU:0, one launch (start us, length us, event | category | flops | bytes accessed | tf_op | source)
XLA Modules:
  0.0 601.0 jit_solution(14945582079892933239)
XLA Ops:
  7.2 0.7 broadcast_add_fusion
  7.9 0.8 copy.138
  8.7 0.7 broadcast_compare_fusion
  10.0 9.1 %gather_fusion.1 = s32[672]{0:T(1024)S(1)} fusion(s32[32,64,3]{1,0,2:T(8,128)S(1)} %copy-done, s32[672]{0:T(1024)S(1)} %reshape.205), kind=kCustom, calls=%fused_computation.1 | custom fusion | bytes 13440 | tf_op jit(solution)/shard_map/jit(take_along_axis)/gather | solution.py:44
  20.2 56.0 %gather_fusion = bf16[1376,2048]{1,0:T(8,128)(2,1)} fusion(bf16[8016,2048]{1,0:T(8,128)(2,1)} %param.16, s32[2048]{0:T(1024)S(1)} %pad_clamp_fusion), kind=kCustom, calls=%fused_computation | custom fusion | bytes 11277696 | tf_op jit(solution)/shard_map/jit(_take)/gather | solution.py:86
  76.2 7.0 %select_convert_fusion = bf16[1376,2048]{1,0:T(8,128)(2,1)} fusion(bf16[1376,2048]{1,0:T(8,128)(2,1)} %gather_fusion, pred[1376]{0:T(1024)(128)(4,1)S(1)} %compare_and_fusion.1, pred[1376]{0:T(1024)(128)(4,1)S(1)} %and.29), kind=kLoop, calls=%fused_computation.9 | loop fusion | flops 11272192 | bytes 11274944 | tf_op jit(solution)/shard_map/convert_element_type | solution.py:89
  83.2 60.9 %fusion = bf16[176,2048]{1,0:T(8,128)(2,1)S(1)} fusion(bf16[1376,2048]{1,0:T(8,128)(2,1)} %select_convert_fusion), kind=kCustom, calls=%all-reduce-scatter | all-reduce-scatter fusion | flops 2883585 | bytes 6357504
  144.1 1.3 collective-permute-start
  146.7 1.5 concatenate.24
  148.2 1.0 constant_dynamic-slice_fusion
  149.3 0.7 all-gather.9.cloned.1.call-update
  150.0 0.7 all-gather.11.cloned.1.call-update
  151.3 3.1 copy.134
  154.4 0.7 fusion.41
  155.1 0.7 fusion.40
  155.8 0.7 fusion.39
  156.4 0.7 fusion.38
  157.1 0.7 fusion.37
  157.8 0.7 fusion.36
  158.4 0.7 fusion.35
  159.1 0.7 fusion.34
  159.8 0.7 fusion.33
  160.4 0.7 fusion.32
  161.1 0.7 fusion.31
  161.8 0.7 fusion.30
  162.4 0.7 fusion.29
  163.1 0.7 fusion.28
  163.7 0.7 fusion.27
  164.4 0.7 fusion.26
  165.1 0.7 fusion.25
  165.7 0.7 fusion.24
  166.4 0.7 fusion.23
  167.1 0.7 fusion.22
  167.7 0.7 fusion.21
  168.4 0.7 fusion.20
  169.1 0.7 fusion.19
  169.7 0.7 fusion.18
  170.4 0.7 fusion.17
  171.1 0.7 fusion.16
  171.7 0.7 fusion.15
  172.4 0.7 fusion.14
  173.0 0.7 fusion.13
  175.7 10.1 %all-to-all-start = ((bf16[32,1,2,4,64,128]{5,4,2,3,1,0:T(8,128)(2,1)}), bf16[32,1,2,4,64,128]{5,4,2,3,1,0:T(8,128)(2,1)}, u32[]{:S(2)}, u32[]{:S(2)}) async-start(bf16[32,1,2,4,64,128]{5,4,2,3,1,0:T(8,128)(2,1)} %fusion.10), calls=%async_computation | async-start | bytes 8388608 | tf_op jit(solution)/shard_map/all_to_all | solution.py:124
  185.8 5.6 copy.149
  191.4 112.3 %all-to-all-done = bf16[32,1,2,4,64,128]{5,4,2,3,1,0:T(8,128)(2,1)} async-done(((bf16[32,1,2,4,64,128]{5,4,2,3,1,0:T(8,128)(2,1)}), bf16[32,1,2,4,64,128]{5,4,2,3,1,0:T(8,128)(2,1)}, u32[]{:S(2)}, u32[]{:S(2)}) %all-to-all-start) | async-done | bytes 4194336 | tf_op jit(solution)/shard_map/all_to_all | solution.py:124
  303.7 3.9 all-to-all-start.1
  308.2 2.6 fusion.4
  310.9 4.3 fusion.54
  315.3 58.0 %all-gather.11.cloned.1.call-done = bf16[8192,256]{1,0:T(8,128)(2,1)} async-done(((bf16[1024,256]{1,0:T(8,128)(2,1)}), bf16[8192,256]{1,0:T(8,128)(2,1)}) %all-gather.11.cloned.1.call-update) | async-done | bytes 4194320 | tf_op jit(solution)/shard_map/all_gather | solution.py:99
  373.2 3.2 convolution_convert_fusion
  376.7 5.4 copy.135
  382.1 20.3 %all-to-all-done.1 = bf16[32,2,4,64,128]{4,3,1,2,0:T(8,128)(2,1)} async-done(((bf16[32,2,4,64,128]{4,3,1,2,0:T(8,128)(2,1)}), bf16[32,2,4,64,128]{4,3,1,2,0:T(8,128)(2,1)}, u32[]{:S(2)}, u32[]{:S(2)}) %all-to-all-start.1) | async-done | bytes 4194336 | tf_op jit(solution)/shard_map/all_to_all | solution.py:132
  402.4 3.3 copy.150
  405.9 2.6 copy.154
  409.1 2.3 copy.155
  411.4 132.2 %all-gather.7.cloned.1.call-done = bf16[8192,2048]{1,0:T(8,128)(2,1)} async-done(((bf16[1024,2048]{1,0:T(8,128)(2,1)}), bf16[8192,2048]{1,0:T(8,128)(2,1)}) %all-gather.7.cloned.1.call-update) | async-done | bytes 33554448 | tf_op jit(solution)/shard_map/all_gather | solution.py:97
  543.6 13.7 %fusion.56 = f32[172,2048]{1,0:T(8,128)S(1)} fusion(bf16[8192,2048]{1,0:T(8,128)(2,1)} %all-gather.7.cloned.1.call-done, bf16[172,8192]{1,0:T(8,128)(2,1)S(1)} %copy-done.6, f32[172]{0:T(256)S(1)} %add_rsqrt_fusion), kind=kOutput, calls=%fused_computation.124 | convolution fusion | flops 5775589376 | bytes 37782192 | tf_op jit(solution)/shard_map/dot_general | solution.py:102
  557.7 0.7 subtract_convert_fusion
  558.8 1.1 copy-done.3
  559.9 10.6 %bitcast_reduce_fusion = (f32[4,2,8,43]{3,2,1,0:T(8,128)S(1)}, f32[4,2,2048,43,8]{2,3,4,1,0:T(8,128)}) fusion(pred[4,2048]{1,0:T(4,128)(4,1)S(1)} %iota_compare_fusion, bf16[2,4,2048,128,1]{3,2,4,0,1:T(8,128)(2,1)S(1)} %bitcast.195, bf16[4,43,2,8,64]{4,1,3,2,0:T(8,128)(2,1)S(1)} %bitcast.234, bf16[4,43,2,8,64]{4,1,3,2,0:T(8,128)(2,1)S(1)} %bitcast.232), kind=kOutput, calls=%fused_computation.3 | convolution fusion | flops 1461155072 | bytes 27462400 | tf_op jit(solution)/shard_map/stkgd,kscd->skgtc/dot_general | solution.py:139
  570.5 1.1 fusion.59
  572.1 9.6 %fusion.2 = f32[4,2,8,43]{3,2,1,0:T(8,128)S(1)} fusion(f32[4,2,2048,43,8]{2,3,4,1,0:T(8,128)} %get-tuple-element.24, f32[4,2,8,43]{3,2,1,0:T(8,128)S(1)} %max.12, pred[4,2048]{1,0:T(4,128)(4,1)S(1)} %iota_compare_fusion), kind=kLoop, calls=%fused_computation.7 | loop fusion | flops 22541632 | bytes 22574592 | tf_op jit(solution)/shard_map/reduce_sum | solution.py:154
  581.6 10.9 %fusion.3 = f32[4,2,8,43,128]{4,3,2,1,0:T(8,128)S(1)} fusion(bf16[2,4,2048,128,1]{3,2,4,0,1:T(8,128)(2,1)S(1)} %bitcast.230, f32[4,2,2048,43,8]{2,3,4,1,0:T(8,128)} %get-tuple-element.24, f32[4,2,8,43]{3,2,1,0:T(8,128)S(1)} %add.84, f32[4,2,8,43]{3,2,1,0:T(8,128)S(1)} %max.12, pred[4,2048]{1,0:T(4,128)(4,1)S(1)} %iota_compare_fusion), kind=kOutput, calls=%fused_computation.8 | convolution fusion | flops 1471021056 | bytes 28177920 | tf_op jit(solution)/shard_map/skgtc,kscd->stkgd/dot_general | solution.py:159
  593.3 1.2 reshape.196
  (71 shorter events, 8.7 us)
Async XLA Ops:
  7.2 2.8 copy-start
  7.2 301.0 %all-gather.5.cloned.1.call-start = ((), (), s32[]{:S(2)}) async-start(), calls=%async_computation.2 | async-start | bytes 3604480 | tf_op jit(solution)/shard_map/all_gather | solution.py:91
  10.0 9.6 %copy-start.7 = (s32[32,22]{0,1:T(8,128)S(1)}, s32[32,22]{0,1:T(8,128)}, u32[]{:S(2)}) copy-start(s32[32,22]{0,1:T(8,128)} %param.12) | copy-start | bytes 8452
  83.2 62.3 %copy-start.10 = (u32[32]{0:T(128)S(1)}, u32[32]{0:T(128)}, u32[]{:S(2)}) copy-start(u32[32]{0:T(128)} %constant.86) | copy-start | bytes 388
  144.1 2.6 collective-permute-start
  149.2 161.6 %all-gather.9.cloned.1.call-start = ((), (), s32[]{:S(2)}) async-start(), calls=%async_computation.4 | async-start | bytes 4718592 | tf_op jit(solution)/shard_map/all_gather | solution.py:98
  150.0 223.2 %all-gather.11.cloned.1.call-start = ((), (), s32[]{:S(2)}) async-start(), calls=%async_computation.5 | async-start | bytes 4718592 | tf_op jit(solution)/shard_map/all_gather | solution.py:99
  150.7 392.9 %all-gather.7.cloned.1.call-start = ((), (), s32[]{:S(2)}) async-start(), calls=%async_computation.3 | async-start | bytes 37748736 | tf_op jit(solution)/shard_map/all_gather | solution.py:97
  175.7 128.0 %all-to-all-start = ((bf16[32,1,2,4,64,128]{5,4,2,3,1,0:T(8,128)(2,1)}), bf16[32,1,2,4,64,128]{5,4,2,3,1,0:T(8,128)(2,1)}, u32[]{:S(2)}, u32[]{:S(2)}) async-start(bf16[32,1,2,4,64,128]{5,4,2,3,1,0:T(8,128)(2,1)} %fusion.10), calls=%async_computation | async-start | bytes 8388608 | tf_op jit(solution)/shard_map/all_to_all | solution.py:124
  303.7 3.9 copy-start.9
  303.7 3.9 copy-start.11
  303.7 98.8 %all-to-all-start.1 = ((bf16[32,2,4,64,128]{4,3,1,2,0:T(8,128)(2,1)}), bf16[32,2,4,64,128]{4,3,1,2,0:T(8,128)(2,1)}, u32[]{:S(2)}, u32[]{:S(2)}) async-start(bf16[32,2,4,64,128]{4,3,1,2,0:T(8,128)(2,1)} %bitcast.228), calls=%async_computation.1 | async-start | bytes 8388608 | tf_op jit(solution)/shard_map/all_to_all | solution.py:132
  310.8 62.4 %copy-start.6 = (bf16[172,8192]{1,0:T(8,128)(2,1)S(1)}, bf16[172,8192]{1,0:T(8,128)(2,1)}, u32[]{:S(2)}) copy-start(bf16[172,8192]{1,0:T(8,128)(2,1)} %all-gather.5.cloned.1.call-done) | copy-start | bytes 8454148
  402.4 3.4 copy-start.2
  405.8 3.3 copy-start.4
  557.7 2.2 copy-start.3
  559.9 10.6 %copy-start.8 = (pred[43,43]{0,1:T(8,128)(4,1)S(1)}, pred[43,43]{0,1:T(8,128)(4,1)}, u32[]{:S(2)}) copy-start(pred[43,43]{0,1:T(8,128)(4,1)} %constant.63.clone) | copy-start | bytes 5551
  572.1 9.6 %copy-start.5 = (bf16[1,2,4,32,64,128]{5,4,3,1,2,0:T(8,128)(2,1)S(1)}, bf16[1,2,4,32,64,128]{5,4,3,1,2,0:T(8,128)(2,1)}, u32[]{:S(2)}) copy-start(bf16[1,2,4,32,64,128]{5,4,3,1,2,0:T(8,128)(2,1)} %copy-done.4) | copy-start | bytes 12582916
  592.5 1.9 copy-start.1
Sparse Core Ops, SparseCore 0:
  149.3 96.1 all-gather.4
  247.4 54.4 all-gather.8
  303.8 69.3 all-gather.10
  375.0 168.5 all-gather.6
